TPU v7x, 32 devices: a whole 2x2x4 slice. The times are simulated.
32 devices in a mesh: img: 4 (over x, core), tp: 8 (over z, y).
Axes of the slice: x: 2, y: 2, z: 4, core: 2. Of those that a mesh axis runs over, the one named last changes fastest.
Arguments:
- patch_tokens: bfloat16 [4096, 1024], P(('img', 'tp')), may hold values from -12 to 12
- norm_gain: float32 [1024], replicated, may hold values from 0.1 to 1.9
- norm_bias: float32 [1024], replicated, may hold values from -3 to 3
- up_weight: bfloat16 [1024, 8192], P('img', 'tp'), may hold values from -0.1875 to 0.1875
- up_bias: float32 [8192], P('tp'), may hold values from -3 to 3
- down_weight: bfloat16 [8192, 4096], P('tp', 'img'), may hold values from -0.125 to 0.125
- down_bias: float32 [4096], replicated, may hold values from -3 to 3
Outputs:
- projected: bfloat16 [4096, 4096], P(('img', 'tp'))
All inputs are finite; a program needn't handle non-finite values.
Results may differ from a plain program's by a relative error of at most 0.014.
Values may be sent and summed in bfloat16 or wider, within the bound.
A program may use at most 128 MiB of HBM per device.

v0:
```python
import jax
import jax.numpy as jnp
from jax import lax
from jax.sharding import PartitionSpec as P


def on_device(patch_tokens, norm_gain, norm_bias, up_weight, up_bias, down_weight, down_bias):
    values = lax.all_gather(patch_tokens, "tp", axis=0, tiled=True).astype(jnp.float32)
    center = jnp.mean(values, axis=1, keepdims=True)
    spread = jnp.mean((values - center) ** 2, axis=1, keepdims=True)
    gathered = ((values - center) * lax.rsqrt(spread + 1e-05) * norm_gain + norm_bias).astype(
        jnp.bfloat16
    )
    summed = jnp.dot(
        gathered,
        lax.all_gather(up_weight, "img", axis=0, tiled=True),
        preferred_element_type=jnp.float32,
    )
    hidden = jax.nn.gelu(summed + up_bias).astype(jnp.bfloat16)
    down_full = lax.all_gather(down_weight, "img", axis=1, tiled=True)
    total = lax.psum_scatter(
        jnp.dot(hidden, down_full, preferred_element_type=jnp.float32).astype(jnp.bfloat16),
        "tp",
        scatter_dimension=0,
        tiled=True,
    ).astype(jnp.float32)
    return (total + down_bias).astype(jnp.bfloat16)


def solution(mesh):
    return jax.shard_map(
        on_device,
        mesh=mesh,
        in_specs=(P(("img", "tp"), None), P(), P(), P("img", "tp"), P("tp"), P("tp", "img"), P()),
        out_specs=P(("img", "tp"), None),
        check_vma=False,
    )
```

profile of v0, /device:TPU:0, one launch (start us, length us, event | category | flops | bytes accessed | tf_op | source)
XLA Modules:
  0.0 318.9 jit_solution(16244446734320534299)
XLA Ops:
  6.5 0.0 copy-start.2
  6.5 0.0 copy-start.4
  6.5 0.0 all-gather.4.cloned.1.call-start
  6.5 0.7 all-gather.4.cloned.1.call-update
  7.3 0.0 all-gather.6.cloned.1.call-start
  7.3 0.7 all-gather.6.cloned.1.call-update
  8.0 0.0 all-gather.8.cloned.1.call-start
  8.1 0.7 all-gather.8.cloned.1.call-update
  8.7 0.0 reduce-scatter.2.cloned.1.call-start
  8.8 52.5 %all-gather.4.cloned.1.call-done = bf16[1024,1024]{1,0:T(8,128)(2,1)} async-done(((bf16[128,1024]{1,0:T(8,128)(2,1)}), bf16[1024,1024]{1,0:T(8,128)(2,1)}) %all-gather.4.cloned.1.call-update) | async-done | bytes 2097168 | tf_op jit(solution)/shard_map/all_gather | solution.py:8
  61.3 0.0 copy-start
  61.3 2.1 convert_reduce_fusion
  63.4 2.3 fusion.2
  65.7 18.3 %all-gather.6.cloned.1.call-done = bf16[1024,1024]{1,0:T(8,128)(2,1)} async-done(((bf16[256,1024]{1,0:T(8,128)(2,1)}), bf16[1024,1024]{1,0:T(8,128)(2,1)}) %all-gather.6.cloned.1.call-update) | async-done | bytes 2097168 | tf_op jit(solution)/shard_map/all_gather | solution.py:16
  84.0 59.9 %all-gather.8.cloned.1.call-done = bf16[1024,4096]{1,0:T(8,128)(2,1)} async-done(((bf16[1024,1024]{1,0:T(8,128)(2,1)}), bf16[1024,4096]{1,0:T(8,128)(2,1)}) %all-gather.8.cloned.1.call-update) | async-done | bytes 8388624 | tf_op jit(solution)/shard_map/all_gather | solution.py:20
  143.9 0.0 copy-done.2
  143.9 0.0 copy-done.3
  143.9 0.0 copy-done.4
  143.9 0.0 copy-done
  143.9 18.4 %convolution_convert_fusion = bf16[1024,4096]{1,0:T(8,128)(2,1)} fusion(bf16[1024,4096]{1,0:T(8,128)(2,1)} %all-gather.8.cloned.1.call-done, bf16[1024,1024]{1,0:T(8,128)(2,1)} %all-gather.6.cloned.1.call-done, bf16[1024,1024]{1,0:T(8,128)(2,1)S(1)} %copy-done, f32[1024]{0:T(1024)S(1)} %copy-done.2, f32[1024]{0:T(1024)S(1)} %copy-done.3, ...), kind=kOutput, calls=%fused_computation | convolution fusion | flops 10758389760 | bytes 20992000 | tf_op jit(solution)/shard_map/dot_general | solution.py:22
  162.3 0.0 reduce-scatter.2.cloned.1.call-update
  162.3 147.6 %reduce-scatter.2.cloned.1.call-done = bf16[128,4096]{1,0:T(8,128)(2,1)} async-done(((bf16[1024,4096]{1,0:T(8,128)(2,1)}), bf16[128,4096]{1,0:T(8,128)(2,1)}) %reduce-scatter.2.cloned.1.call-update) | async-done | bytes 1048592 | tf_op jit(solution)/shard_map/reduce_scatter | solution.py:21
  309.9 0.0 copy-done.1
  310.0 2.4 add_convert_fusion
  (4 shorter events, 0.0 us)
Async XLA Ops:
  6.5 137.3 %copy-start.2 = (f32[1024]{0:T(1024)S(1)}, f32[1024]{0:T(1024)}, u32[]{:S(2)}) copy-start(f32[1024]{0:T(1024)} %param.11) | copy-start | bytes 12292
  6.5 137.3 %copy-start.3 = (f32[1024]{0:T(1024)S(1)}, f32[1024]{0:T(1024)}, u32[]{:S(2)}) copy-start(f32[1024]{0:T(1024)} %param.9) | copy-start | bytes 12292
  6.5 137.3 %copy-start.4 = (f32[1024]{0:T(1024)S(1)}, f32[1024]{0:T(1024)}, u32[]{:S(2)}) copy-start(f32[1024]{0:T(1024)} %param.8) | copy-start | bytes 12292
  6.5 54.8 %all-gather.4.cloned.1.call-start = ((), (), s32[]{:S(2)}) async-start(), calls=%async_computation.1 | async-start | bytes 2359296 | tf_op jit(solution)/shard_map/all_gather | solution.py:8
  7.3 76.7 %all-gather.6.cloned.1.call-start = ((), (), s32[]{:S(2)}) async-start(), calls=%async_computation.2 | async-start | bytes 2621440 | tf_op jit(solution)/shard_map/all_gather | solution.py:16
  8.0 135.8 %all-gather.8.cloned.1.call-start = ((), (), s32[]{:S(2)}) async-start(), calls=%async_computation.3 | async-start | bytes 10485760 | tf_op jit(solution)/shard_map/all_gather | solution.py:20
  8.7 301.2 %reduce-scatter.2.cloned.1.call-start = ((), (), s32[]{:S(2)}) async-start(), calls=%async_computation.4 | async-start | bytes 9437184 | tf_op jit(solution)/shard_map/reduce_scatter | solution.py:21
  61.3 82.6 %copy-start = (bf16[1024,1024]{1,0:T(8,128)(2,1)S(1)}, bf16[1024,1024]{1,0:T(8,128)(2,1)}, u32[]{:S(2)}) copy-start(bf16[1024,1024]{1,0:T(8,128)(2,1)} %all-gather.4.cloned.1.call-done) | copy-start | bytes 6291460
  162.3 147.7 %copy-start.1 = (f32[4096]{0:T(1024)S(1)}, f32[4096]{0:T(1024)}, u32[]{:S(2)}) copy-start(f32[4096]{0:T(1024)} %param.13) | copy-start | bytes 49156
Sparse Core Ops, SparseCore 0:
  9.5 51.7 all-gather.3
  62.9 21.0 all-gather.5
  85.6 58.2 all-gather.7
  162.4 147.4 reduce-scatter.1
where the time goes:
time: 319 us
  waiting for transfers between devices  280 us (88%)
  matrix products  18.4 us (6%)
  between operations  13.1 us (4%)
  other arithmetic  6.78 us (2%)
    reduce_scatter x1, waiting for transfers between devices, on_device(): lax.psum_scatter(jnp.dot(hidden, down_full, preferred_element_type=jnp.fl...  148 us
    all_gather x1, waiting for transfers between devices, on_device(): down_full = lax.all_gather(down_weight, 'img', axis=1, tiled=True)  59.9 us
    all_gather x1, waiting for transfers between devices, on_device(): lax.all_gather(patch_tokens, 'tp', axis=0, tiled=True).astype(jnp.float32)  52.5 us
    dot_general x1, matrix products, on_device(): jnp.dot(hidden, down_full, preferred_element_type=jnp.float32)  18.4 us
    all_gather x1, waiting for transfers between devices, on_device(): lax.all_gather(up_weight, 'img', axis=0, tiled=True)  18.3 us
  transfers between devices with their start and end apart: 4, of which 4 were waited for; matrix products, arithmetic and copies ran while one was open for 1% of the time, Pallas kernels for 0%

commit v1 on v0

v1 whole, which is shorter than its diff:
```python
import functools

import jax
import jax.numpy as jnp
from jax import lax
from jax.experimental import pallas as pl
from jax.experimental.pallas import tpu as pltpu
from jax.sharding import PartitionSpec as P

MESH = pl.DeviceIdType.MESH
LANES = 128
UP_STAGES = 2


def kernel(n_img, n_tp, x_ref, gain_ref, nbias_ref, up_ref, ubias_ref, down_ref, dbias_ref, out_ref,
           tok, normed, upf, ubf, hidden, dn, pb, rb,
           tk_s, tk_r, bs_s, bs_r, own_sem, dx_s, dx_r, dm_s, dm_r, r1_s, r1_r, r2_s, r2_r,
           p_s, p_r, rs_s, rs_r):
    cores = 2 if n_img % 2 == 0 else 1
    pair = 2 if n_tp % 2 == 0 else 1
    n_x, n_g = n_img // cores, n_tp // pair
    img, tp = lax.axis_index("img"), lax.axis_index("tp")
    x, c = img // cores, img % cores
    g, m = tp // pair, tp % pair
    rows, width = x_ref.shape
    depth, units = up_ref.shape
    n_chunk = down_ref.shape[1] // LANES
    u_rows = depth // UP_STAGES
    stages = UP_STAGES + n_chunk

    def at_x(k):
        return {"img": lax.rem(x + k, n_x) * cores + c, "tp": tp}

    def at_m(k):
        return {"img": img, "tp": g * pair + lax.rem(m + k, pair)}

    def at_g(k):
        return {"img": img, "tp": lax.rem(g + k, n_g) * pair + m}

    partner = {"img": x * cores + (cores - 1 - c), "tp": tp}
    xs, ms, gs = range(1, n_x), range(1, pair), range(1, n_g)

    def is_up(s):
        return isinstance(s, int) and s < UP_STAGES

    def source(s):
        if is_up(s):
            return up_ref.at[pl.ds(s * u_rows, u_rows), :]
        return down_ref.at[:, pl.ds(pl.multiple_of((s - UP_STAGES) * LANES, LANES), LANES)]

    def block(s, kx, km, core, half=None):
        src = lax.rem(x - kx + n_x, n_x) * cores + core
        src_m = lax.rem(m - km + pair, pair)
        if is_up(s):
            size, lo = u_rows, src * depth + s * u_rows
            if half is not None:
                size, lo = u_rows // 2, lo + half * (u_rows // 2)
            return upf.at[src_m, pl.ds(pl.multiple_of(lo, size), size), :]
        size, lo = units, src_m * units
        if half is not None:
            size, lo = units // 2, lo + half * (units // 2)
        return dn.at[s - UP_STAGES, pl.ds(pl.multiple_of(lo, size), size),
                     pl.ds(pl.multiple_of(src * LANES, LANES), LANES)]

    def copy(src, dst, send, recv, device):
        return pltpu.make_async_remote_copy(
            src_ref=src, dst_ref=dst, send_sem=send, recv_sem=recv,
            device_id=device, device_id_type=MESH)

    def direct_x(s, k, src, dst):
        return copy(src, dst, dx_s.at[s, k], dx_r.at[s, k], at_x(k))

    def direct_m(s, k, src, dst):
        return copy(src, dst, dm_s.at[s, k], dm_r.at[s, k], at_m(k))

    def relay_m(s, kx, km, ref):
        return copy(ref, ref, r1_s.at[s, kx, km], r1_r.at[s, kx, km], at_m(km))

    def relay_x(s, kx, km, ref):
        return copy(ref, ref, r2_s.at[s, kx, km], r2_r.at[s, kx, km], at_x(kx))

    def across(s, kx, km, src, dst):
        return copy(src, dst, p_s.at[s, kx, km], p_r.at[s, kx, km], partner)

    def own_copy(s):
        return pltpu.make_async_copy(source(s), block(s, 0, 0, c), own_sem.at[s])

    def issue(s):
        here, place = source(s), block(s, 0, 0, c)
        for k in xs:
            direct_x(s, k, here, place).start()
        for k in ms:
            direct_m(s, k, here, place).start()
        if cores > 1:
            across(s, 0, 0, here, place).start()
        own_copy(s).start()

    def forward(s):
        for k in xs:
            ref = block(s, k, 0, c)
            direct_x(s, k, ref, ref).wait_recv()
            for km in ms:
                relay_m(s, k, km, block(s, k, 0, c, 0)).start()
            if cores > 1:
                across(s, k, 0, ref, ref).start()
        for km in ms:
            ref = block(s, 0, km, c)
            direct_m(s, km, ref, ref).wait_recv()
            for k in xs:
                relay_x(s, k, km, block(s, 0, km, c, 1)).start()
            if cores > 1:
                across(s, 0, km, ref, ref).start()

    def collect(s):
        for k in xs:
            for km in ms:
                relay_m(s, k, km, block(s, k, km, c, 0)).wait_recv()
                relay_x(s, k, km, block(s, k, km, c, 1)).wait_recv()
                if cores > 1:
                    ref = block(s, k, km, c)
                    across(s, k, km, ref, ref).start()
        own_copy(s).wait()
        if cores > 1:
            for k in range(n_x):
                for km in range(pair):
                    ref = block(s, k, km, cores - 1 - c)
                    across(s, k, km, ref, ref).wait_recv()

    def finish(s):
        for k in xs:
            direct_x(s, k, source(s), source(s)).wait_send()
        for km in ms:
            direct_m(s, km, source(s), source(s)).wait_send()
        for k in xs:
            for km in ms:
                relay_m(s, k, km, block(s, k, 0, c, 0)).wait_send()
                relay_x(s, k, km, block(s, 0, km, c, 1)).wait_send()
        if cores > 1:
            for k in range(n_x):
                for km in range(pair):
                    ref = block(s, k, km, c)
                    across(s, k, km, ref, ref).wait_send()

    def token(k, src, slot):
        return copy(src, tok.at[slot], tk_s.at[k], tk_r.at[k], at_g(k))

    def bias(k, src, slot):
        return copy(src, ubf.at[slot], bs_s.at[k], bs_r.at[k], at_m(k))

    def partial(j, k, src):
        return copy(src, rb.at[j, k - 1], rs_s.at[j, k], rs_r.at[j, k], at_g(k))

    def normalize(values, at):
        values = values.astype(jnp.float32)
        center = jnp.mean(values, axis=1, keepdims=True)
        spread = jnp.mean((values - center) ** 2, axis=1, keepdims=True)
        lines = (values - center) * lax.rsqrt(spread + 1e-05) * gain_ref[...] + nbias_ref[...]
        normed[pl.ds(pl.multiple_of(at * rows, rows), rows), :] = lines.astype(jnp.bfloat16)

    barrier = pltpu.get_barrier_semaphore()
    near = [at_x(k) for k in xs] + [at_m(k) for k in ms] + [at_g(k) for k in gs]
    if cores > 1:
        near.append(partner)
    for device in near:
        pl.semaphore_signal(barrier, inc=1, device_id=device, device_id_type=MESH)
    pl.semaphore_wait(barrier, len(near))

    for k in gs:
        token(k, x_ref, k - 1).start()
    for k in ms:
        bias(k, ubias_ref, k - 1).start()
    issue(0)
    issue(1)
    normalize(x_ref[...], g)

    forward(0)
    issue(2)
    for k in gs:
        token(k, x_ref, k - 1).wait_recv()
        normalize(tok[k - 1], lax.rem(g - k + n_g, n_g))
    for k in ms:
        bias(k, ubias_ref, k - 1).wait_recv()
    forward(1)
    if stages > 3:
        issue(3)
    collect(0)
    forward(2)
    if stages > 4:
        issue(4)
    collect(1)

    tile = 256
    per_m = units // tile

    for km in range(pair):
        place = lax.rem(m - km + pair, pair)
        biases = ubias_ref if km == 0 else ubf.at[km - 1]

        def up_tile(n, carry):
            cols = pl.ds(pl.multiple_of(n * tile, tile), tile)
            summed = jnp.dot(normed[...], upf[place, :, cols], preferred_element_type=jnp.float32)
            wide = pl.ds(pl.multiple_of(place * units + n * tile, tile), tile)
            hidden[:, wide] = jax.nn.gelu(summed + biases[:, cols]).astype(jnp.bfloat16)
            return carry

        lax.fori_loop(0, per_m, up_tile, 0)

    def multiply(j):
        def down_tile(n, carry):
            cols = pl.ds(pl.multiple_of(n * tile, tile), tile)
            value = jnp.dot(hidden[...], dn[j, :, cols], preferred_element_type=jnp.float32)
            pb[j, :, :, cols] = value.reshape(n_g, rows, tile).astype(jnp.bfloat16)
            return carry

        lax.fori_loop(0, n_img * LANES // tile, down_tile, 0)
        for k in gs:
            partial(j, k, pb.at[j, lax.rem(g + k, n_g)]).start()

    def tick(s, carry):
        @pl.when(s < stages)
        def _():
            forward(s)

        @pl.when(s + 2 < stages)
        def _():
            issue(s + 2)

        collect(s - 1)
        multiply(s - 1 - UP_STAGES)
        return carry

    lax.fori_loop(UP_STAGES + 1, stages + 1, tick, 0)

    def reduce(j, carry):
        total = pb[j, g].astype(jnp.float32)
        for k in gs:
            partial(j, k, pb.at[j, 0]).wait_recv()
            total += rb[j, k - 1].astype(jnp.float32)
        for i in range(n_img):
            cols = pl.ds(pl.multiple_of((i * n_chunk + j) * LANES, LANES), LANES)
            part = total[:, i * LANES:(i + 1) * LANES] + dbias_ref[:, cols]
            out_ref[:, cols] = part.astype(jnp.bfloat16)
        for k in gs:
            partial(j, k, pb.at[j, 0]).wait_send()
        return carry

    lax.fori_loop(0, n_chunk, reduce, 0)
    for s in range(UP_STAGES):
        finish(s)

    def finish_tick(s, carry):
        finish(s)
        return carry

    lax.fori_loop(UP_STAGES, stages, finish_tick, 0)
    for k in gs:
        token(k, x_ref, k - 1).wait_send()
    for k in ms:
        bias(k, ubias_ref, k - 1).wait_send()


def solution(mesh):
    n_img, n_tp = mesh.shape["img"], mesh.shape["tp"]
    cores = 2 if n_img % 2 == 0 else 1
    pair = 2 if n_tp % 2 == 0 else 1
    n_x, n_g = n_img // cores, n_tp // pair

    def on_device(x, gain, nbias, up, ubias, down, dbias):
        rows, width = x.shape
        depth, units = up.shape
        n_chunk = down.shape[1] // LANES
        stages = UP_STAGES + n_chunk
        wide = n_img * LANES
        bf16 = jnp.bfloat16
        dma = pltpu.SemaphoreType.DMA
        scratch = [
            pltpu.VMEM((max(n_g - 1, 1), rows, width), bf16),
            pltpu.VMEM((n_g * rows, width), bf16),
            pltpu.VMEM((pair, width, units), bf16),
            pltpu.VMEM((max(pair - 1, 1), 1, units), jnp.float32),
            pltpu.VMEM((n_g * rows, pair * units), bf16),
            pltpu.VMEM((n_chunk, pair * units, wide), bf16),
            pltpu.VMEM((n_chunk, n_g, rows, wide), bf16),
            pltpu.VMEM((n_chunk, max(n_g - 1, 1), rows, wide), bf16),
        ]
        scratch += [dma((n_g,))] * 2 + [dma((pair,))] * 2 + [dma((stages,))]
        scratch += [dma((stages, n_x))] * 2 + [dma((stages, pair))] * 2
        scratch += [dma((stages, n_x, pair))] * 6 + [dma((n_chunk, n_g))] * 2
        return pl.pallas_call(
            functools.partial(kernel, n_img, n_tp),
            out_shape=jax.ShapeDtypeStruct((rows, n_img * down.shape[1]), bf16),
            in_specs=[pl.BlockSpec(memory_space=pltpu.VMEM)] * 7,
            out_specs=pl.BlockSpec(memory_space=pltpu.VMEM),
            scratch_shapes=scratch,
            compiler_params=pltpu.CompilerParams(
                collective_id=0, has_side_effects=True, vmem_limit_bytes=60 * 1024 * 1024),
        )(x, gain.reshape(1, -1), nbias.reshape(1, -1), up, ubias.reshape(1, -1), down,
          dbias.reshape(1, -1))

    return jax.shard_map(
        on_device,
        mesh=mesh,
        in_specs=(P(("img", "tp"), None), P(), P(), P("img", "tp"), P("tp"), P("tp", "img"), P()),
        out_specs=P(("img", "tp"), None),
        check_vma=False,
    )
```

time: 319 us -> 143 us (0.45)
  the two profiles are of different devices: /device:TPU:0 before, /device:TPU:27 now
where the time goes in v1:
time: 143 us; the launch traced here: 142 us
  Pallas kernels  140 us (98%)
  local copies, waits for them, and re-layouts  2.29 us (2%)
    pallas_call x1, Pallas kernels, on_device(): pl.pallas_call(functools.partial(kernel, n_img, n_tp), out_shape=jax.Shap...  140 us

profile of v1, /device:TPU:27, one launch (start us, length us, event | category | flops | bytes accessed | tf_op | source)
XLA Modules:
  0.0 142.3 jit_solution(17905404556046957133)
XLA Ops:
  0.0 140.0 %shard_map.73 = bf16[128,4096]{1,0:T(8,128)(2,1)} custom-call(bf16[128,1024]{1,0:T(8,128)(2,1)} %x_ref.1, f32[1,1024]{1,0:T(1,128)} %bitcast.5, f32[1,1024]{1,0:T(1,128)} %bitcast.6, bf16[256,1024]{1,0:T(8,128)(2,1)} %up_ref.1, f32[1,1024]{1,0:T(1,128)} %bitcast.7, bf16[1024,1024]{1,0:T(8,128)(2,1)} %down_ref.1, f32[1,4096]{1,0:T(1,128)} %bitcast.4), custom_call_target="tpu_custom_call" | custom-call | tf_op jit(solution)/shard_map/pallas_call | solution.py:289
  140.0 2.3 %copy.9 = bf16[128,4096]{1,0:T(8,128)(2,1)} copy(bf16[128,4096]{1,0:T(8,128)(2,1)} %shard_map.73) | data formatting | bytes 2097152

commit v2 on v1

--- a/solution.py
+++ b/solution.py
@@ -13,9 +13,9 @@
 
 
 def kernel(n_img, n_tp, x_ref, gain_ref, nbias_ref, up_ref, ubias_ref, down_ref, dbias_ref, out_ref,
-           tok, normed, upf, ubf, hidden, dn, pb, rb,
+           tok, normed, upf, ubf, hidden, dn, pb, from_low, from_high, sums,
            tk_s, tk_r, bs_s, bs_r, own_sem, dx_s, dx_r, dm_s, dm_r, r1_s, r1_r, r2_s, r2_r,
-           p_s, p_r, rs_s, rs_r):
+           p_s, p_r, lo_s, lo_r, hi_s, hi_r):
     cores = 2 if n_img % 2 == 0 else 1
     pair = 2 if n_tp % 2 == 0 else 1
     n_x, n_g = n_img // cores, n_tp // pair
@@ -147,8 +147,11 @@
     def bias(k, src, slot):
         return copy(src, ubf.at[slot], bs_s.at[k], bs_r.at[k], at_m(k))
 
-    def partial(j, k, src):
-        return copy(src, rb.at[j, k - 1], rs_s.at[j, k], rs_r.at[j, k], at_g(k))
+    def upward(j, d):
+        return copy(pb.at[j, d], from_low.at[j, d], lo_s.at[j, d], lo_r.at[j, d], at_g(1))
+
+    def downward(j, d):
+        return copy(pb.at[j, d], from_high.at[j, d], hi_s.at[j, d], hi_r.at[j, d], at_g(n_g - 1))
 
     def normalize(values, at):
         values = values.astype(jnp.float32)
@@ -213,8 +216,32 @@
             return carry
 
         lax.fori_loop(0, n_img * LANES // tile, down_tile, 0)
-        for k in gs:
-            partial(j, k, pb.at[j, lax.rem(g + k, n_g)]).start()
+
+    def pass_on(step):
+        j_up, j_down = step - g, step - (n_g - 1 - g)
+        go_up = (g < n_g - 1) & (j_up >= 0) & (j_up < n_chunk)
+        go_down = (g > 0) & (j_down >= 0) & (j_down < n_chunk)
+
+        def accumulate(j, d, copies, arrived):
+            copies(j, d).wait_recv()
+            pb[j, d] = (pb[j, d].astype(jnp.float32) + arrived[j, d].astype(jnp.float32)).astype(jnp.bfloat16)
+
+        for d in reversed(range(1, n_g)):
+            @pl.when(go_up & (g > 0) & (g < d))
+            def _():
+                accumulate(j_up, d, upward, from_low)
+        for d in range(n_g - 1):
+            @pl.when(go_down & (g < n_g - 1) & (g > d))
+            def _():
+                accumulate(j_down, d, downward, from_high)
+        for d in reversed(range(1, n_g)):
+            @pl.when(go_up & (g < d))
+            def _():
+                upward(j_up, d).start()
+        for d in range(n_g - 1):
+            @pl.when(go_down & (g > d))
+            def _():
+                downward(j_down, d).start()
 
     def tick(s, carry):
         @pl.when(s < stages)
@@ -225,26 +252,54 @@
         def _():
             issue(s + 2)
 
+        step = s - 1 - UP_STAGES
         collect(s - 1)
-        multiply(s - 1 - UP_STAGES)
-        return carry
-
-    lax.fori_loop(UP_STAGES + 1, stages + 1, tick, 0)
-
-    def reduce(j, carry):
+        multiply(step)
+        pass_on(step)
+
+        @pl.when(step >= n_g)
+        def _():
+            reduce(step - n_g)
+        return carry
+
+    def reduce(j):
         total = pb[j, g].astype(jnp.float32)
-        for k in gs:
-            partial(j, k, pb.at[j, 0]).wait_recv()
-            total += rb[j, k - 1].astype(jnp.float32)
         for i in range(n_img):
             cols = pl.ds(pl.multiple_of((i * n_chunk + j) * LANES, LANES), LANES)
-            part = total[:, i * LANES:(i + 1) * LANES] + dbias_ref[:, cols]
-            out_ref[:, cols] = part.astype(jnp.bfloat16)
-        for k in gs:
-            partial(j, k, pb.at[j, 0]).wait_send()
-        return carry
-
-    lax.fori_loop(0, n_chunk, reduce, 0)
+            piece = slice(i * LANES, (i + 1) * LANES)
+            sums[:, piece] = total[:, piece] + dbias_ref[:, cols]
+        for first, copies, arrived in ((g > 0, upward, from_low), (g < n_g - 1, downward, from_high)):
+            @pl.when(first)
+            def _():
+                copies(j, g).wait_recv()
+                sums[...] += arrived[j, g].astype(jnp.float32)
+        for i in range(n_img):
+            cols = pl.ds(pl.multiple_of((i * n_chunk + j) * LANES, LANES), LANES)
+            out_ref[:, cols] = sums[:, i * LANES:(i + 1) * LANES].astype(jnp.bfloat16)
+
+    def drain(step, carry):
+        pass_on(step)
+        return carry
+
+    def reduce_tick(j, carry):
+        reduce(j)
+        return carry
+
+    def sent(j, carry):
+        for d in range(n_g):
+            @pl.when(g < d)
+            def _():
+                upward(j, d).wait_send()
+
+            @pl.when(g > d)
+            def _():
+                downward(j, d).wait_send()
+        return carry
+
+    lax.fori_loop(UP_STAGES + 1, stages + 1, tick, 0)
+    lax.fori_loop(n_chunk, n_chunk + n_g - 2, drain, 0)
+    lax.fori_loop(max(n_chunk - n_g, 0), n_chunk, reduce_tick, 0)
+    lax.fori_loop(0, n_chunk, sent, 0)
     for s in range(UP_STAGES):
         finish(s)
 
@@ -281,11 +336,13 @@
             pltpu.VMEM((n_g * rows, pair * units), bf16),
             pltpu.VMEM((n_chunk, pair * units, wide), bf16),
             pltpu.VMEM((n_chunk, n_g, rows, wide), bf16),
-            pltpu.VMEM((n_chunk, max(n_g - 1, 1), rows, wide), bf16),
+            pltpu.VMEM((n_chunk, n_g, rows, wide), bf16),
+            pltpu.VMEM((n_chunk, n_g, rows, wide), bf16),
+            pltpu.VMEM((rows, wide), jnp.float32),
         ]
         scratch += [dma((n_g,))] * 2 + [dma((pair,))] * 2 + [dma((stages,))]
         scratch += [dma((stages, n_x))] * 2 + [dma((stages, pair))] * 2
-        scratch += [dma((stages, n_x, pair))] * 6 + [dma((n_chunk, n_g))] * 2
+        scratch += [dma((stages, n_x, pair))] * 6 + [dma((n_chunk, n_g))] * 4
         return pl.pallas_call(
             functools.partial(kernel, n_img, n_tp),
             out_shape=jax.ShapeDtypeStruct((rows, n_img * down.shape[1]), bf16),

time: 143 us -> 132 us (0.923)
  the two profiles are of different devices: /device:TPU:27 before, /device:TPU:0 now
where the time goes in v2:
time: 132 us
  Pallas kernels  129 us (98%)
  local copies, waits for them, and re-layouts  2.29 us (2%)
    pallas_call x1, Pallas kernels, on_device(): pl.pallas_call(functools.partial(kernel, n_img, n_tp), out_shape=jax.Shap...  129 us

profile of v2, /device:TPU:0, one launch (start us, length us, event | category | flops | bytes accessed | tf_op | source)
XLA Modules:
  0.0 131.5 jit_solution(16268506300406207244)
XLA Ops:
  0.0 129.2 %shard_map.73 = bf16[128,4096]{1,0:T(8,128)(2,1)} custom-call(bf16[128,1024]{1,0:T(8,128)(2,1)} %x_ref.1, f32[1,1024]{1,0:T(1,128)} %bitcast.5, f32[1,1024]{1,0:T(1,128)} %bitcast.6, bf16[256,1024]{1,0:T(8,128)(2,1)} %up_ref.1, f32[1,1024]{1,0:T(1,128)} %bitcast.7, bf16[1024,1024]{1,0:T(8,128)(2,1)} %down_ref.1, f32[1,4096]{1,0:T(1,128)} %bitcast.4), custom_call_target="tpu_custom_call" | custom-call | tf_op jit(solution)/shard_map/pallas_call | solution.py:346
  129.2 2.3 %copy.9 = bf16[128,4096]{1,0:T(8,128)(2,1)} copy(bf16[128,4096]{1,0:T(8,128)(2,1)} %shard_map.73) | data formatting | bytes 2097152

commit v3 on v2

--- a/solution.py
+++ b/solution.py
@@ -178,11 +178,6 @@
 
     forward(0)
     issue(2)
-    for k in gs:
-        token(k, x_ref, k - 1).wait_recv()
-        normalize(tok[k - 1], lax.rem(g - k + n_g, n_g))
-    for k in ms:
-        bias(k, ubias_ref, k - 1).wait_recv()
     forward(1)
     if stages > 3:
         issue(3)
@@ -190,6 +185,11 @@
     forward(2)
     if stages > 4:
         issue(4)
+    for k in gs:
+        token(k, x_ref, k - 1).wait_recv()
+        normalize(tok[k - 1], lax.rem(g - k + n_g, n_g))
+    for k in ms:
+        bias(k, ubias_ref, k - 1).wait_recv()
     collect(1)
 
     tile = 256
@@ -226,22 +226,24 @@
             copies(j, d).wait_recv()
             pb[j, d] = (pb[j, d].astype(jnp.float32) + arrived[j, d].astype(jnp.float32)).astype(jnp.bfloat16)
 
-        for d in reversed(range(1, n_g)):
-            @pl.when(go_up & (g > 0) & (g < d))
-            def _():
-                accumulate(j_up, d, upward, from_low)
-        for d in range(n_g - 1):
-            @pl.when(go_down & (g < n_g - 1) & (g > d))
-            def _():
-                accumulate(j_down, d, downward, from_high)
-        for d in reversed(range(1, n_g)):
-            @pl.when(go_up & (g < d))
-            def _():
-                upward(j_up, d).start()
-        for d in range(n_g - 1):
-            @pl.when(go_down & (g > d))
-            def _():
-                downward(j_down, d).start()
+        for k in range(n_g - 1):
+            high, low = n_g - 1 - k, k
+
+            @pl.when(go_up & (g > 0) & (g < high))
+            def _():
+                accumulate(j_up, high, upward, from_low)
+
+            @pl.when(go_down & (g < n_g - 1) & (g > low))
+            def _():
+                accumulate(j_down, low, downward, from_high)
+
+            @pl.when(go_up & (g < high))
+            def _():
+                upward(j_up, high).start()
+
+            @pl.when(go_down & (g > low))
+            def _():
+                downward(j_down, low).start()
 
     def tick(s, carry):
         @pl.when(s < stages)

time: 132 us -> 123 us (0.932)
  Pallas kernels: 129 us -> 120 us
    pallas_call x1, Pallas kernels: 129 us -> 120 us  [on_device(): pl.pallas_call(functools.partial(kernel, n_img, n_tp), out_shape=jax.Shap...]
where the time goes in v3:
time: 123 us; the launch traced here: 122 us
  Pallas kernels  120 us (98%)
  local copies, waits for them, and re-layouts  2.29 us (2%)
    pallas_call x1, Pallas kernels, on_device(): pl.pallas_call(functools.partial(kernel, n_img, n_tp), out_shape=jax.Shap...  120 us

profile of v3, /device:TPU:0, one launch (start us, length us, event | category | flops | bytes accessed | tf_op | source)
XLA Modules:
  0.0 122.5 jit_solution(3807968154897473095)
XLA Ops:
  0.0 120.2 %shard_map.73 = bf16[128,4096]{1,0:T(8,128)(2,1)} custom-call(bf16[128,1024]{1,0:T(8,128)(2,1)} %x_ref.1, f32[1,1024]{1,0:T(1,128)} %bitcast.5, f32[1,1024]{1,0:T(1,128)} %bitcast.6, bf16[256,1024]{1,0:T(8,128)(2,1)} %up_ref.1, f32[1,1024]{1,0:T(1,128)} %bitcast.7, bf16[1024,1024]{1,0:T(8,128)(2,1)} %down_ref.1, f32[1,4096]{1,0:T(1,128)} %bitcast.4), custom_call_target="tpu_custom_call" | custom-call | tf_op jit(solution)/shard_map/pallas_call | solution.py:348
  120.2 2.3 %copy.9 = bf16[128,4096]{1,0:T(8,128)(2,1)} copy(bf16[128,4096]{1,0:T(8,128)(2,1)} %shard_map.73) | data formatting | bytes 2097152
